TPU v7x, 32 devices: a whole 2x2x4 slice. The times are simulated.
32 devices in a mesh: leaf: 8 (over z, x), blk: 4 (over y, core).
Axes of the slice: x: 2, y: 2, z: 4, core: 2. Of those that a mesh axis runs over, the one named last changes fastest.
Arguments:
- desc_panel: bfloat16 [256, 384, 128], P(('leaf', 'blk')), may hold values from -18 to 18
- row_map: int32 [256, 3], P(('leaf', 'blk')), may hold values from 0 to 55, as said below
- anc_order: int32 [8], replicated, may hold values from 0 to 7, as said below
- anc_below: int32 [8, 12], replicated, may hold values from 32 to 55, as said below
- anc_panel: float32 [8, 4, 4, 128, 512], P('leaf', None, 'blk'), may hold values from -6 to 27, as said below
Outputs:
- chol_panel: float32 [8, 4, 4, 128, 512], P('leaf', None, 'blk')
Inputs may be any that keep to these rules, and one draw needn't show every extreme that they name: `row_map`: entry 0 of each row is a column block of one ancestor; the other entries are distinct entries of that ancestor's row of anc_below. Over the descendants of one device, entry 0 names the column blocks of any one ancestor at most 2 times, and of some ancestor exactly 2 times. `anc_order`: each leaf index holds a different column range. `anc_below`: each row holds 12 distinct indices. `anc_panel`: the leading 512 rows of each ancestor's panel are symmetric, and the leading block of S stays positive definite.
All inputs are finite; a program needn't handle non-finite values.
Results may differ from a plain program's by a relative error of at most 0.0003.
Values may be sent and summed in bfloat16 or wider, within the bound.
A program may use at most 192 MiB of HBM per device.

v0:
```python
import jax
import jax.numpy as jnp
from jax import lax
from jax.sharding import PartitionSpec as P

SLOTS = 2
slot_group = 16


def leaf_owner(ranges, anc_order):
    leaves = jnp.arange(anc_order.shape[0], dtype=jnp.int32)
    return jnp.sum(jnp.where(anc_order[None, :] == ranges[:, None], leaves[None, :], 0), axis=1)


def block_positions(block_ids, owner_leaf, anc_order, anc_below, column_blocks, position_count):
    column_base = anc_order[owner_leaf] * column_blocks
    relative = block_ids - column_base[:, None]
    in_columns = (relative >= 0) & (relative < column_blocks)
    below_ids = anc_below[owner_leaf]
    matching = block_ids[:, :, None] == below_ids[:, None, :]
    offsets = column_blocks + jnp.arange(below_ids.shape[1], dtype=jnp.int32)
    below_place = jnp.sum(jnp.where(matching, offsets[None, None, :], 0), axis=2)
    located = jnp.any(matching, axis=2)
    return jnp.where(in_columns, relative, jnp.where(located, below_place, position_count))


def place_blocks(running, group_place, group_products):
    return running + jnp.einsum(
        "kq,kxy->qxy", group_place, group_products, precision=lax.Precision.HIGHEST
    )


def shards(desc_panel, row_map, anc_order, anc_below, anc_panel):
    leaf_count = lax.axis_size("leaf")
    blk_count = lax.axis_size("blk")
    desc_count, block_count = row_map.shape
    block_rows = anc_panel.shape[3]
    panel_width = anc_panel.shape[4]
    wide_desc = desc_panel.shape[2]
    column_blocks = panel_width // block_rows
    position_count = column_blocks + anc_below.shape[1]
    slot_count = leaf_count * SLOTS
    group_count = slot_count // slot_group
    owner_leaf = leaf_owner(row_map[:, 0] // column_blocks, anc_order)
    positions = block_positions(
        row_map, owner_leaf, anc_order, anc_below, column_blocks, position_count
    )
    desc_index = jnp.arange(desc_count, dtype=jnp.int32)
    same_owner = owner_leaf[:, None] == owner_leaf[None, :]
    earlier = desc_index[None, :] < desc_index[:, None]
    ranking = jnp.sum(same_owner & earlier, axis=1)
    slot_of = owner_leaf * SLOTS + ranking
    matches = slot_of[None, :] == jnp.arange(slot_count, dtype=jnp.int32)[:, None]
    filled = jnp.any(matches, axis=1)
    chosen = jnp.sum(jnp.where(matches, desc_index[None, :], 0), axis=1)
    picked = jnp.where(filled, chosen, desc_count)
    slot_codes = jnp.where(filled[:, None], positions[chosen], position_count).reshape(
        leaf_count, SLOTS, block_count
    )
    send_rows = jnp.take(desc_panel, picked, axis=0, mode="fill", fill_value=0)
    send_rows = send_rows.reshape(leaf_count, SLOTS, block_count * block_rows, wide_desc)
    received, received_codes = (
        lax.all_to_all(send_rows, "leaf", split_axis=0, concat_axis=0, tiled=True),
        lax.all_to_all(
            slot_codes.astype(jnp.bfloat16), "leaf", split_axis=0, concat_axis=0, tiled=True
        ),
    )
    slot_data = received.reshape(group_count, slot_group, block_count * block_rows, wide_desc)

    def accumulate(running, element):
        group_data, group_place = element
        products = jnp.einsum(
            "kaw,kyw->kay",
            group_data,
            group_data[:, :block_rows],
            preferred_element_type=jnp.float32,
        )
        products = products.reshape(slot_group * block_count, block_rows, block_rows)
        return (place_blocks(running, group_place, products), None)

    codes_int = received_codes.astype(jnp.int32).reshape(slot_count, block_count)
    target = codes_int * column_blocks + codes_int[:, :1]
    placing = (
        target[:, :, None]
        == jnp.arange(position_count * column_blocks, dtype=jnp.int32)[None, None, :]
    ).astype(jnp.float32)
    placing = placing.reshape(group_count, slot_group * block_count, position_count * column_blocks)
    initial = jnp.zeros((position_count * column_blocks, block_rows, block_rows), jnp.float32)
    running, _ = lax.scan(accumulate, initial, (slot_data, placing))
    update = running.reshape(position_count, column_blocks, block_rows, block_rows).transpose(
        0, 2, 1, 3
    )
    update = update.reshape(position_count // blk_count, blk_count, block_rows, panel_width)
    local_rows = anc_panel[0]
    mine = lax.axis_index("blk")
    marker = (jnp.arange(blk_count, dtype=jnp.int32) == mine).astype(jnp.float32)
    combined = update - local_rows * marker[None, :, None, None]
    summed = lax.psum(combined, "blk")
    diagonal = -summed.reshape(position_count * block_rows, panel_width)[:panel_width]
    own_rows = -lax.dynamic_slice_in_dim(summed, mine, 1, 1)
    lower_factor = jnp.linalg.cholesky(diagonal)
    panel_rows = own_rows.reshape(-1, panel_width)
    solved = jax.scipy.linalg.solve_triangular(lower_factor, panel_rows.T, lower=True).T
    return solved.reshape(anc_panel.shape)


def solution(mesh):
    in_specs = (
        P(("leaf", "blk"), None, None),
        P(("leaf", "blk"), None),
        P(),
        P(),
        P("leaf", None, "blk", None, None),
    )
    out_specs = P("leaf", None, "blk", None, None)
    return jax.shard_map(shards, mesh=mesh, in_specs=in_specs, out_specs=out_specs, check_vma=False)
```

profile of v0, /device:TPU:0, one launch (start us, length us, event | category | flops | bytes accessed | tf_op | source)
XLA Modules:
  0.0 327.3 jit_solution(11401863305329569041)
XLA Ops:
  6.5 0.8 fusion.45
  7.3 0.8 select_reduce_fusion.5
  8.5 0.8 copy.53
  9.4 1.3 gather_fusion
  10.7 1.2 gather_fusion.1
  11.9 0.9 compare_reduce_fusion
  12.8 0.9 fusion.40
  14.0 0.6 gather_fusion.2
  14.8 0.7 copy.58
  15.5 7.3 %all-to-all-start = ((bf16[8,2,3]{2,1,0:T(2,128)(2,1)}), bf16[8,2,3]{2,1,0:T(2,128)(2,1)S(1)}, u32[]{:S(2)}, u32[]{:S(2)}) async-start(bf16[8,2,3]{2,1,0:T(2,128)(2,1)} %copy.58), calls=%async_computation | async-start | bytes 8192 | tf_op jit(solution)/shard_map/all_to_all | solution.py:64
  22.8 0.9 gather_fusion.3
  23.7 1.3 broadcast_select_fusion
  25.0 4.1 %all-to-all-done = bf16[8,2,3]{2,1,0:T(2,128)(2,1)S(1)} async-done(((bf16[8,2,3]{2,1,0:T(2,128)(2,1)}), bf16[8,2,3]{2,1,0:T(2,128)(2,1)S(1)}, u32[]{:S(2)}, u32[]{:S(2)}) %all-to-all-start) | async-done | bytes 128 | tf_op jit(solution)/shard_map/all_to_all | solution.py:64
  29.2 3.6 %all-to-all-start.1 = ((bf16[8,2,384,128]{3,2,1,0:T(8,128)(2,1)}), bf16[8,2,384,128]{3,2,1,0:T(8,128)(2,1)S(1)}, u32[]{:S(2)}, u32[]{:S(2)}) async-start(bf16[8,2,384,128]{3,2,1,0:T(8,128)(2,1)} %broadcast_select_fusion), calls=%async_computation.1 | async-start | bytes 3145728 | tf_op jit(solution)/shard_map/all_to_all | solution.py:63
  32.8 1.6 copy.62
  34.8 33.9 %all-to-all-done.1 = bf16[8,2,384,128]{3,2,1,0:T(8,128)(2,1)S(1)} async-done(((bf16[8,2,384,128]{3,2,1,0:T(8,128)(2,1)}), bf16[8,2,384,128]{3,2,1,0:T(8,128)(2,1)S(1)}, u32[]{:S(2)}, u32[]{:S(2)}) %all-to-all-start.1) | async-done | bytes 1572896 | tf_op jit(solution)/shard_map/all_to_all | solution.py:63
  68.7 0.6 fusion.12
  69.3 6.0 %fusion.3 = f32[16,128,4,128]{3,0,1,2:T(8,128)} fusion(f32[48,128,128]{2,1,0:T(8,128)S(1)} %bitcast.107, s32[16,4]{0,1:T(4,128)S(1)} %multiply_add_fusion, s32[48]{0:T(128)S(1)} %add.130), kind=kOutput, calls=%fused_computation.10 | convolution fusion | flops 603982848 | bytes 7340480 | tf_op jit(solution)/shard_map/while/body/eval_jaxpr/kq,kxy->qxy/dot_general | solution.py:28
  75.3 5.7 %copy.61 = f32[16,128,4,128]{1,3,2,0:T(8,128)} copy(f32[16,128,4,128]{3,0,1,2:T(8,128)} %fusion.3) | data formatting | bytes 8388608 | tf_op jit(solution)/shard_map/transpose | solution.py:90
  80.9 4.7 %multiply_subtract_fusion = f32[4,4,128,512]{2,3,1,0:T(8,128)} fusion(f32[4,4,128,512]{2,3,1,0:T(8,128)} %bitcast.106, f32[4]{0:T(128)S(1)} %compare_convert_fusion, f32[4,128,512]{1,2,0:T(8,128)S(1)} %copy.62), kind=kLoop, calls=%fused_computation.6 | loop fusion | flops 2097152 | bytes 9437200 | tf_op jit(solution)/shard_map/sub | solution.py:97
  85.7 84.5 %all-reduce.3.cloned.1.call-done = f32[4,4,128,512]{2,3,1,0:T(8,128)} async-done(((f32[4,4,128,512]{2,3,1,0:T(8,128)}), f32[4,4,128,512]{2,3,1,0:T(8,128)}) %all-reduce.3.cloned.1.call-update) | async-done | bytes 4194320 | tf_op jit(solution)/shard_map/psum | solution.py:98
  170.1 1.3 slice_negate_fusion
  171.4 0.7 copy.63
  172.1 1.0 copy.84
  173.2 1.6 copy.64
  174.7 0.2 fusion.6
  175.0 1.0 copy-done.2
  175.9 11.7 %cholesky.104 = f32[128,128]{1,0:T(8,128)S(1)} custom-call(f32[128,128]{1,0:T(8,128)S(1)} %cholesky.266), custom_call_target="Cholesky" | custom-call | tf_op jit(solution)/shard_map/jit(cholesky)/cholesky | solution.py:101
  187.8 9.8 %custom-call.31 = f32[1,128,128]{1,2,0:T(8,128)S(1)} custom-call(f32[1,128,128]{2,1,0:T(8,128)S(1)} %get-tuple-element.44), custom_call_target="InvertDiagBlocksLowerTriangular" | custom-call | tf_op jit(solution)/shard_map/jit(cholesky)/cholesky | solution.py:101
  197.6 1.2 constant_dynamic-update-slice_fusion.3
  198.9 1.3 convolution_subtract_fusion.3
  200.1 11.9 %cholesky.217 = f32[128,128]{1,0:T(8,128)S(1)} custom-call(f32[128,128]{1,0:T(8,128)S(1)} %cholesky.270), custom_call_target="Cholesky" | custom-call | tf_op jit(solution)/shard_map/jit(cholesky)/cholesky | solution.py:101
  212.0 0.7 compare_reduce_fusion.3
  212.7 0.6 compare_reduce_fusion.4
  213.4 9.8 %custom-call.32 = f32[1,128,128]{1,2,0:T(8,128)S(1)} custom-call(f32[1,128,128]{2,1,0:T(8,128)S(1)} %get-tuple-element.41), custom_call_target="InvertDiagBlocksLowerTriangular" | custom-call | tf_op jit(solution)/shard_map/jit(cholesky)/cholesky | solution.py:101
  223.2 0.3 convolution_dynamic-update-slice_fusion
  223.4 1.3 convolution_subtract_fusion.4
  224.7 11.7 %cholesky.238 = f32[128,128]{1,0:T(8,128)S(1)} custom-call(f32[128,128]{1,0:T(8,128)S(1)} %cholesky.275), custom_call_target="Cholesky" | custom-call | tf_op jit(solution)/shard_map/jit(cholesky)/cholesky | solution.py:101
  236.5 0.7 compare_reduce_fusion.2
  237.2 9.8 %custom-call.33 = f32[1,128,128]{1,2,0:T(8,128)S(1)} custom-call(f32[1,128,128]{2,1,0:T(8,128)S(1)} %get-tuple-element.38), custom_call_target="InvertDiagBlocksLowerTriangular" | custom-call | tf_op jit(solution)/shard_map/jit(cholesky)/cholesky | solution.py:101
  247.2 1.2 convolution_subtract_fusion.5
  248.5 11.9 %cholesky.255 = f32[128,128]{1,0:T(8,128)S(1)} custom-call(f32[128,128]{1,0:T(8,128)S(1)} %convolution_subtract_fusion.5), custom_call_target="Cholesky" | custom-call | tf_op jit(solution)/shard_map/jit(cholesky)/cholesky | solution.py:101
  260.4 0.6 compare_reduce_fusion.1
  263.8 7.9 %while.1 = (s32[]{:T(128)}, f32[512,512]{1,0:T(8,128)S(1)}, s32[4,2]{0,1:T(2,128)S(1)}, f32[4,128,128]{2,1,0:T(8,128)S(1)}, s32[]{:T(128)}) while((s32[]{:T(128)}, f32[512,512]{1,0:T(8,128)S(1)}, s32[4,2]{0,1:T(2,128)S(1)}, f32[4,128,128]{2,1,0:T(8,128)S(1)}, s32[]{:T(128)}) %tuple.30), condition=%wide.while_cond, body=%wide.while_body.sunk | while | flops 2 | bytes 131181 | solution.py:103
  263.9 0.5 fusion.57
  264.4 1.4 bitcast_dynamic-update-slice_fusion.2
  265.8 0.5 fusion.57
  266.4 1.4 bitcast_dynamic-update-slice_fusion.2
  267.8 0.5 fusion.57
  268.3 1.4 bitcast_dynamic-update-slice_fusion.2
  269.8 0.5 fusion.57
  270.3 1.4 bitcast_dynamic-update-slice_fusion.2
  271.7 39.3 %custom-call.34 = f32[4,128,128]{1,2,0:T(8,128)S(1)} custom-call(f32[4,128,128]{2,1,0:T(8,128)S(1)} %get-tuple-element.24), custom_call_target="InvertDiagBlocksLowerTriangular" | custom-call | tf_op jit(solution)/shard_map/jit(_solve_triangular)/triangular_solve | solution.py:103
  311.0 1.3 dynamic-slice_negate_fusion
  312.3 0.3 copy.65
  312.7 0.3 copy.66
  313.0 0.4 fusion.17
  313.4 1.2 convolution_subtract_fusion.1
  314.6 0.4 fusion.30
  315.1 1.3 convolution_subtract_fusion
  316.4 0.4 fusion.28
  316.8 1.6 convolution_subtract_fusion.2
  318.4 0.4 fusion.27
  318.9 1.3 copy.72
  (53 shorter events, 2.4 us)
Async XLA Ops:
  6.5 16.3 %copy-start = (bf16[8,384,128]{2,1,0:T(8,128)(2,1)S(1)}, bf16[8,384,128]{2,1,0:T(8,128)(2,1)}, u32[]{:S(2)}) copy-start(bf16[8,384,128]{2,1,0:T(8,128)(2,1)} %param.5) | copy-start | bytes 2359300
  15.5 13.7 %all-to-all-start = ((bf16[8,2,3]{2,1,0:T(2,128)(2,1)}), bf16[8,2,3]{2,1,0:T(2,128)(2,1)S(1)}, u32[]{:S(2)}, u32[]{:S(2)}) async-start(bf16[8,2,3]{2,1,0:T(2,128)(2,1)} %copy.58), calls=%async_computation | async-start | bytes 8192 | tf_op jit(solution)/shard_map/all_to_all | solution.py:64
  29.2 39.5 %all-to-all-start.1 = ((bf16[8,2,384,128]{3,2,1,0:T(8,128)(2,1)}), bf16[8,2,384,128]{3,2,1,0:T(8,128)(2,1)S(1)}, u32[]{:S(2)}, u32[]{:S(2)}) async-start(bf16[8,2,384,128]{3,2,1,0:T(8,128)(2,1)} %broadcast_select_fusion), calls=%async_computation.1 | async-start | bytes 3145728 | tf_op jit(solution)/shard_map/all_to_all | solution.py:63
  32.7 137.4 %all-reduce.3.cloned.1.call-start = ((), (), s32[]{:S(2)}) async-start(), calls=%async_computation.2 | async-start | bytes 8388608 | tf_op jit(solution)/shard_map/psum | solution.py:98
  174.9 1.0 copy-start.2
  271.7 39.3 %copy-start.1 = (f32[512,512]{1,0:T(8,128)}, f32[512,512]{1,0:T(8,128)S(1)}, u32[]{:S(2)}) copy-start(f32[512,512]{1,0:T(8,128)S(1)} %get-tuple-element.101) | copy-start | bytes 3145732
Sparse Core Ops, SparseCore 0:
  85.8 84.3 all-reduce.2
where the time goes:
time: 333 us; the launch traced here: 327 us
  other arithmetic  132 us (40%)
  waiting for transfers between devices  123 us (37%)
  local copies, waits for them, and re-layouts  27.7 us (8%)
  matrix products  17.8 us (5%)
  between operations  16.6 us (5%)
  starting transfers between devices  10.9 us (3%)
    psum x1, waiting for transfers between devices, shards(): summed = lax.psum(combined, 'blk')  84.5 us
    another operation x15, other arithmetic, shards(): lower_factor = jnp.linalg.cholesky(diagonal)  79.4 us
    another operation x3, other arithmetic, shards(): jax.scipy.linalg.solve_triangular(lower_factor, panel_rows.T, lower=True)  39.4 us
    all_to_all x1, waiting for transfers between devices, shards(): lax.all_to_all(send_rows, 'leaf', split_axis=0, concat_axis=0, tiled=True)  33.9 us
    another operation x12, local copies, waits for them, and re-layouts  7.81 us
    all_to_all x1, starting transfers between devices, shards(): lax.all_to_all(slot_codes.astype(jnp.bfloat16), 'leaf', split_axis=0, con...  7.28 us
  transfers between devices with their start and end apart: 3, of which 3 were waited for; matrix products, arithmetic and copies ran while one was open for 1% of the time, Pallas kernels for 0%

commit v1 on v0

--- a/solution.py
+++ b/solution.py
@@ -95,7 +95,7 @@
     mine = lax.axis_index("blk")
     marker = (jnp.arange(blk_count, dtype=jnp.int32) == mine).astype(jnp.float32)
     combined = update - local_rows * marker[None, :, None, None]
-    summed = lax.psum(combined, "blk")
+    summed = jnp.sum(lax.all_gather(combined, "blk"), axis=0)
     diagonal = -summed.reshape(position_count * block_rows, panel_width)[:panel_width]
     own_rows = -lax.dynamic_slice_in_dim(summed, mine, 1, 1)
     lower_factor = jnp.linalg.cholesky(diagonal)

time: 333 us -> 371 us (1.11)
  waiting for transfers between devices: 123 us -> 143 us
  local copies, waits for them, and re-layouts: 27.7 us -> 36.7 us
  other arithmetic: 132 us -> 139 us
    all_gather x0 -> x1, waiting for transfers between devices: none -> 105 us  [shards(): summed = jnp.sum(lax.all_gather(combined, 'blk'), axis=0)]
    psum x1 -> x0, waiting for transfers between devices: 84.5 us -> none  [shards(): summed = lax.psum(combined, 'blk')]
    reduce_sum x0 -> x1, other arithmetic: none -> 10.3 us  [shards(): summed = jnp.sum(lax.all_gather(combined, 'blk'), axis=0)]
    sub x0 -> x1, local copies, waits for them, and re-layouts: none -> 5.68 us  [shards(): combined = update - local_rows * marker[None, :, None, None]]
where the time goes in v1:
time: 371 us; the launch traced here: 365 us
  waiting for transfers between devices  143 us (39%)
  other arithmetic  139 us (37%)
  local copies, waits for them, and re-layouts  36.7 us (10%)
  matrix products  18 us (5%)
  between operations  16.6 us (4%)
  starting transfers between devices  10.9 us (3%)
    all_gather x1, waiting for transfers between devices, shards(): summed = jnp.sum(lax.all_gather(combined, 'blk'), axis=0)  105 us
    another operation x15, other arithmetic, shards(): lower_factor = jnp.linalg.cholesky(diagonal)  79.2 us
    another operation x3, other arithmetic, shards(): jax.scipy.linalg.solve_triangular(lower_factor, panel_rows.T, lower=True)  39.4 us
    all_to_all x1, waiting for transfers between devices, shards(): lax.all_to_all(send_rows, 'leaf', split_axis=0, concat_axis=0, tiled=True)  33.9 us
    reduce_sum x1, other arithmetic, shards(): summed = jnp.sum(lax.all_gather(combined, 'blk'), axis=0)  10.3 us
    another operation x12, local copies, waits for them, and re-layouts  8.39 us
  transfers between devices with their start and end apart: 3, of which 3 were waited for; matrix products, arithmetic and copies ran while one was open for 1% of the time, Pallas kernels for 0%

profile of v1, /device:TPU:0, one launch (start us, length us, event | category | flops | bytes accessed | tf_op | source)
XLA Modules:
  0.0 364.7 jit_solution(12782355200673824989)
XLA Ops:
  6.5 0.8 fusion.45
  7.3 0.8 select_reduce_fusion.5
  8.5 0.8 copy.55
  9.4 1.3 gather_fusion
  10.7 1.2 gather_fusion.1
  11.9 0.9 compare_reduce_fusion
  12.8 0.9 fusion.40
  14.0 0.6 gather_fusion.2
  14.8 0.7 copy.60
  15.5 7.3 %all-to-all-start = ((bf16[8,2,3]{2,1,0:T(2,128)(2,1)}), bf16[8,2,3]{2,1,0:T(2,128)(2,1)S(1)}, u32[]{:S(2)}, u32[]{:S(2)}) async-start(bf16[8,2,3]{2,1,0:T(2,128)(2,1)} %copy.60), calls=%async_computation | async-start | bytes 8192 | tf_op jit(solution)/shard_map/all_to_all | solution.py:64
  22.8 0.9 gather_fusion.3
  23.7 1.3 broadcast_select_fusion
  25.0 4.1 %all-to-all-done = bf16[8,2,3]{2,1,0:T(2,128)(2,1)S(1)} async-done(((bf16[8,2,3]{2,1,0:T(2,128)(2,1)}), bf16[8,2,3]{2,1,0:T(2,128)(2,1)S(1)}, u32[]{:S(2)}, u32[]{:S(2)}) %all-to-all-start) | async-done | bytes 128 | tf_op jit(solution)/shard_map/all_to_all | solution.py:64
  29.2 3.6 all-to-all-start.1
  32.8 1.6 copy.64
  34.8 33.9 %all-to-all-done.1 = bf16[8,2,384,128]{3,2,1,0:T(8,128)(2,1)S(1)} async-done(((bf16[8,2,384,128]{3,2,1,0:T(8,128)(2,1)}), bf16[8,2,384,128]{3,2,1,0:T(8,128)(2,1)S(1)}, u32[]{:S(2)}, u32[]{:S(2)}) %all-to-all-start.1) | async-done | bytes 1572896 | tf_op jit(solution)/shard_map/all_to_all | solution.py:63
  68.7 0.6 fusion.12
  69.3 6.0 %fusion.3 = f32[16,128,4,128]{3,0,1,2:T(8,128)} fusion(f32[48,128,128]{2,1,0:T(8,128)S(1)} %bitcast.107, s32[16,4]{0,1:T(4,128)S(1)} %multiply_add_fusion, s32[48]{0:T(128)S(1)} %add.128), kind=kOutput, calls=%fused_computation.10 | convolution fusion | flops 603982848 | bytes 7340480 | tf_op jit(solution)/shard_map/while/body/eval_jaxpr/kq,kxy->qxy/dot_general | solution.py:28
  75.3 5.2 %copy.63 = f32[16,128,4,128]{1,3,2,0:T(8,128)} copy(f32[16,128,4,128]{3,0,1,2:T(8,128)} %fusion.3) | data formatting | bytes 8388608 | tf_op jit(solution)/shard_map/transpose | solution.py:90
  80.5 4.7 %multiply_subtract_fusion = f32[1,4,4,128,512]{3,4,2,1,0:T(8,128)} fusion(f32[1,4,4,128,512]{3,4,2,1,0:T(8,128)} %bitcast.106, f32[4]{0:T(128)S(1)} %compare_convert_fusion, f32[4,128,512]{1,2,0:T(8,128)S(1)} %copy.64), kind=kLoop, calls=%fused_computation.6 | loop fusion | flops 2097152 | bytes 9437200 | tf_op jit(solution)/shard_map/sub | solution.py:97
  85.2 5.7 %copy.65 = f32[1,4,4,128,512]{4,3,2,1,0:T(8,128)} copy(f32[1,4,4,128,512]{3,4,2,1,0:T(8,128)} %multiply_subtract_fusion) | data formatting | bytes 8388608 | tf_op jit(solution)/shard_map/sub | solution.py:97
  90.9 104.9 %all-gather.2.cloned.1.call-done = f32[4,4,4,128,512]{4,3,2,1,0:T(8,128)} async-done(((f32[1,4,4,128,512]{4,3,2,1,0:T(8,128)}), f32[4,4,4,128,512]{4,3,2,1,0:T(8,128)}) %all-gather.2.cloned.1.call-update) | async-done | bytes 16777232 | tf_op jit(solution)/shard_map/all_gather | solution.py:98
  195.8 10.3 %reduce_sum.58 = f32[4,4,128,512]{3,2,1,0:T(8,128)} reduce(f32[4,4,4,128,512]{4,3,2,1,0:T(8,128)} %all-gather.2.cloned.1.call-done, f32[]{:T(128)} %constant.201.clone.1), dimensions={0}, to_apply=%region_6.7 | reduce | flops 3145728 | bytes 20971524 | tf_op jit(solution)/shard_map/reduce_sum | solution.py:98
  206.1 1.3 slice.153
  207.8 0.7 copy.67
  208.5 1.0 copy.91
  209.5 1.6 copy.68
  211.3 1.0 copy-done.3
  212.3 11.7 %cholesky.104 = f32[128,128]{1,0:T(8,128)S(1)} custom-call(f32[128,128]{1,0:T(8,128)S(1)} %cholesky.266), custom_call_target="Cholesky" | custom-call | tf_op jit(solution)/shard_map/jit(cholesky)/cholesky | solution.py:101
  224.2 9.8 %custom-call.31 = f32[1,128,128]{1,2,0:T(8,128)S(1)} custom-call(f32[1,128,128]{2,1,0:T(8,128)S(1)} %get-tuple-element.44), custom_call_target="InvertDiagBlocksLowerTriangular" | custom-call | tf_op jit(solution)/shard_map/jit(cholesky)/cholesky | solution.py:101
  234.0 1.2 constant_dynamic-update-slice_fusion.3
  235.2 1.3 convolution_subtract_fusion.3
  236.5 11.9 %cholesky.217 = f32[128,128]{1,0:T(8,128)S(1)} custom-call(f32[128,128]{1,0:T(8,128)S(1)} %cholesky.270), custom_call_target="Cholesky" | custom-call | tf_op jit(solution)/shard_map/jit(cholesky)/cholesky | solution.py:101
  248.4 0.6 compare_reduce_fusion.3
  249.1 0.7 compare_reduce_fusion.4
  249.8 9.8 %custom-call.32 = f32[1,128,128]{1,2,0:T(8,128)S(1)} custom-call(f32[1,128,128]{2,1,0:T(8,128)S(1)} %get-tuple-element.41), custom_call_target="InvertDiagBlocksLowerTriangular" | custom-call | tf_op jit(solution)/shard_map/jit(cholesky)/cholesky | solution.py:101
  259.9 1.3 convolution_subtract_fusion.4
  261.2 11.7 %cholesky.238 = f32[128,128]{1,0:T(8,128)S(1)} custom-call(f32[128,128]{1,0:T(8,128)S(1)} %cholesky.275), custom_call_target="Cholesky" | custom-call | tf_op jit(solution)/shard_map/jit(cholesky)/cholesky | solution.py:101
  272.9 0.7 compare_reduce_fusion.2
  273.6 9.8 %custom-call.33 = f32[1,128,128]{1,2,0:T(8,128)S(1)} custom-call(f32[1,128,128]{2,1,0:T(8,128)S(1)} %get-tuple-element.38), custom_call_target="InvertDiagBlocksLowerTriangular" | custom-call | tf_op jit(solution)/shard_map/jit(cholesky)/cholesky | solution.py:101
  283.6 1.4 convolution_subtract_fusion.5
  285.0 11.7 %cholesky.255 = f32[128,128]{1,0:T(8,128)S(1)} custom-call(f32[128,128]{1,0:T(8,128)S(1)} %convolution_subtract_fusion.5), custom_call_target="Cholesky" | custom-call | tf_op jit(solution)/shard_map/jit(cholesky)/cholesky | solution.py:101
  296.8 0.6 compare_reduce_fusion.1
  300.1 8.5 %while.1 = (s32[]{:T(128)}, f32[512,512]{1,0:T(8,128)S(1)}, s32[4,2]{0,1:T(2,128)S(1)}, f32[4,128,128]{2,1,0:T(8,128)S(1)}, s32[]{:T(128)}) while((s32[]{:T(128)}, f32[512,512]{1,0:T(8,128)S(1)}, s32[4,2]{0,1:T(2,128)S(1)}, f32[4,128,128]{2,1,0:T(8,128)S(1)}, s32[]{:T(128)}) %tuple.30), condition=%wide.while_cond, body=%wide.while_body.sunk | while | flops 2 | bytes 131181 | solution.py:103
  300.2 0.6 fusion.57
  300.8 1.4 bitcast_dynamic-update-slice_fusion.2
  302.3 0.6 fusion.57
  302.9 1.4 bitcast_dynamic-update-slice_fusion.2
  304.4 0.6 fusion.57
  305.0 1.4 bitcast_dynamic-update-slice_fusion.2
  306.6 0.6 fusion.57
  307.2 1.4 bitcast_dynamic-update-slice_fusion.2
  308.6 39.3 %custom-call.34 = f32[4,128,128]{1,2,0:T(8,128)S(1)} custom-call(f32[4,128,128]{2,1,0:T(8,128)S(1)} %get-tuple-element.24), custom_call_target="InvertDiagBlocksLowerTriangular" | custom-call | tf_op jit(solution)/shard_map/jit(_solve_triangular)/triangular_solve | solution.py:103
  347.9 1.3 constant_dynamic-slice_fusion.1
  349.7 0.3 copy.69
  350.0 0.3 copy.70
  350.3 0.4 fusion.17
  350.8 1.2 convolution_subtract_fusion.1
  352.0 0.4 fusion.30
  352.4 1.3 convolution_subtract_fusion
  353.8 0.4 fusion.28
  354.2 1.6 convolution_subtract_fusion.2
  355.8 0.4 fusion.27
  356.3 1.3 copy.76
  (61 shorter events, 3.7 us)
Async XLA Ops:
  6.5 16.3 %copy-start = (bf16[8,384,128]{2,1,0:T(8,128)(2,1)S(1)}, bf16[8,384,128]{2,1,0:T(8,128)(2,1)}, u32[]{:S(2)}) copy-start(bf16[8,384,128]{2,1,0:T(8,128)(2,1)} %param.5) | copy-start | bytes 2359300
  15.5 13.7 %all-to-all-start = ((bf16[8,2,3]{2,1,0:T(2,128)(2,1)}), bf16[8,2,3]{2,1,0:T(2,128)(2,1)S(1)}, u32[]{:S(2)}, u32[]{:S(2)}) async-start(bf16[8,2,3]{2,1,0:T(2,128)(2,1)} %copy.60), calls=%async_computation | async-start | bytes 8192 | tf_op jit(solution)/shard_map/all_to_all | solution.py:64
  29.2 39.5 %all-to-all-start.1 = ((bf16[8,2,384,128]{3,2,1,0:T(8,128)(2,1)}), bf16[8,2,384,128]{3,2,1,0:T(8,128)(2,1)S(1)}, u32[]{:S(2)}, u32[]{:S(2)}) async-start(bf16[8,2,384,128]{3,2,1,0:T(8,128)(2,1)} %broadcast_select_fusion), calls=%async_computation.1 | async-start | bytes 3145728 | tf_op jit(solution)/shard_map/all_to_all | solution.py:63
  32.7 163.0 %all-gather.2.cloned.1.call-start = ((), (), s32[]{:S(2)}) async-start(), calls=%async_computation.2 | async-start | bytes 20971520 | tf_op jit(solution)/shard_map/all_gather | solution.py:98
  211.3 1.0 copy-start.3
  308.6 39.3 %copy-start.2 = (f32[512,512]{1,0:T(8,128)}, f32[512,512]{1,0:T(8,128)S(1)}, u32[]{:S(2)}) copy-start(f32[512,512]{1,0:T(8,128)S(1)} %get-tuple-element.102) | copy-start | bytes 3145732
  353.7 3.8 %copy-start.1 = (bf16[8,384,128]{2,1,0:T(8,128)(2,1)S(1)}, bf16[8,384,128]{2,1,0:T(8,128)(2,1)}, u32[]{:S(2)}) copy-start(bf16[8,384,128]{2,1,0:T(8,128)(2,1)} %param.5) | copy-start | bytes 2359300
Sparse Core Ops, SparseCore 0:
  91.0 104.7 all-gather.1
